TPU v7x, 32 devices: a whole 2x2x4 slice. The times are simulated.
32 devices in a mesh: ctx: 8 (over z, core), head: 4 (over y, x).
Axes of the slice: x: 2, y: 2, z: 4, core: 2. Of those that a mesh axis runs over, the one named last changes fastest.
Arguments:
- queries: bfloat16 [2048, 8192], P(('ctx', 'head')), may hold values from -100 to 100
- keys: bfloat16 [2048, 1024], P(('ctx', 'head')), may hold values from -100 to 100
- values: bfloat16 [2048, 1024], P(('ctx', 'head')), may hold values from -6 to 6
- out_grad: bfloat16 [2048, 8192], P(('ctx', 'head')), may hold values from -6 to 6
- doc_ids: int32 [2048], replicated, may hold values from 0 to 3, never falling along the last dimension, each value on 1 to 1024 neighbouring positions
Outputs:
- query_grad: float32 [2048, 8192], P(('ctx', 'head'))
- key_grad: float32 [2048, 1024], P(('ctx', 'head'))
- value_grad: float32 [2048, 1024], P(('ctx', 'head'))
Inputs may be any that keep to these rules, and one draw needn't show every extreme that they name: `doc_ids`: never falling along the sequence; each document holds 1 to 1024 tokens, one exactly 1024.
All inputs are finite; a program needn't handle non-finite values.
Results may differ from a plain program's by a relative error of at most 0.004.
Values may be sent and summed in bfloat16 or wider, within the bound.
A program may use at most 64 MiB of HBM per device.

v0:
```python
import jax
import jax.numpy as jnp
from jax import lax
from jax.sharding import PartitionSpec as P

HD = 128


def passed_along(array, axis, by):
    size = lax.axis_size(axis)
    pairs = [(i, i + by) for i in range(size) if 0 <= i + by < size]
    return lax.ppermute(array, axis, pairs)


def body(queries, keys, values, out_grad, doc_ids):
    head_count = lax.axis_size("head")
    row_count = queries.shape[0] * head_count
    score_scale = 1.0 / HD**0.5
    query_loc, key_loc, value_loc, grad_loc = (
        lax.all_to_all(queries, "head", split_axis=1, concat_axis=0, tiled=True),
        lax.all_to_all(keys, "head", split_axis=1, concat_axis=0, tiled=True),
        lax.all_to_all(values, "head", split_axis=1, concat_axis=0, tiled=True),
        lax.all_to_all(out_grad, "head", split_axis=1, concat_axis=0, tiled=True),
    )
    kv_local = key_loc.shape[1] // HD
    group_size = query_loc.shape[1] // key_loc.shape[1]
    key_value = jnp.stack([key_loc, value_loc])
    received = [key_value]
    current = key_value
    for stride in range(1, 4):
        current = passed_along(current, "ctx", 1)
        received.append(current)
    window_kv = jnp.concatenate(received[::-1], axis=1)
    key_win = window_kv[0].reshape(4 * row_count, kv_local, HD)
    value_win = window_kv[1].reshape(4 * row_count, kv_local, HD)
    first_row = lax.axis_index("ctx") * row_count
    query_pos = first_row + jnp.arange(row_count, dtype=jnp.int32)
    key_pos = first_row - 3 * row_count + jnp.arange(4 * row_count, dtype=jnp.int32)
    query_doc = lax.dynamic_slice_in_dim(doc_ids, first_row, row_count, 0)
    key_doc = jnp.concatenate(
        [
            lax.dynamic_slice_in_dim(
                doc_ids, jnp.maximum(first_row - stride * row_count, 0), row_count, 0
            )
            for stride in (3, 2, 1, 0)
        ],
        0,
    )
    allowed = (key_pos[None, :] <= query_pos[:, None]) & (
        key_pos[None, :] > query_pos[:, None] - 3 * row_count
    )
    allowed = allowed & (key_pos[None, :] >= 0) & (query_doc[:, None] == key_doc[None, :])
    query_heads = query_loc.reshape(row_count, kv_local, group_size, HD)
    scores = (
        jnp.einsum("ikgd,jkd->kgij", query_heads, key_win, preferred_element_type=jnp.float32)
        * score_scale
    )
    scores = jnp.where(allowed[None, None], scores, -jnp.inf)
    row_max = jnp.max(scores, -1, keepdims=True)
    expo = jnp.exp(scores - row_max)
    weights = expo / jnp.sum(expo, -1, keepdims=True)
    weight_bf = weights.astype(jnp.bfloat16)
    attended = jnp.einsum(
        "kgij,jkd->ikgd", weight_bf, value_win, preferred_element_type=jnp.float32
    )
    grad_heads = grad_loc.reshape(row_count, kv_local, group_size, HD)
    delta_sum = jnp.transpose(jnp.sum(grad_heads.astype(jnp.float32) * attended, -1), (1, 2, 0))
    value_part = jnp.einsum(
        "kgij,ikgd->jkd", weight_bf, grad_heads, preferred_element_type=jnp.float32
    )
    prob_grad = jnp.einsum(
        "ikgd,jkd->kgij", grad_heads, value_win, preferred_element_type=jnp.float32
    )
    score_grad = (weights * (prob_grad - delta_sum[..., None])).astype(jnp.bfloat16)
    query_full = (
        jnp.einsum("kgij,jkd->ikgd", score_grad, key_win, preferred_element_type=jnp.float32)
        * score_scale
    )
    key_part = (
        jnp.einsum("kgij,ikgd->jkd", score_grad, query_heads, preferred_element_type=jnp.float32)
        * score_scale
    )
    partials = jnp.stack([key_part, value_part]).reshape(2, 4 * row_count, kv_local * HD)

    def piece(stride):
        return partials[:, (3 - stride) * row_count : (4 - stride) * row_count]

    total = piece(3)
    for stride in (2, 1, 0):
        total = passed_along(total, "ctx", -1) + piece(stride)
    query_rows = query_full.reshape(row_count, -1)
    query_back, key_back, value_back = (
        lax.all_to_all(query_rows, "head", split_axis=0, concat_axis=1, tiled=True),
        lax.all_to_all(total[0], "head", split_axis=0, concat_axis=1, tiled=True),
        lax.all_to_all(total[1], "head", split_axis=0, concat_axis=1, tiled=True),
    )
    return (query_back, key_back, value_back)


def solution(mesh):
    return jax.shard_map(
        body,
        mesh=mesh,
        in_specs=(
            P(("ctx", "head"), None),
            P(("ctx", "head"), None),
            P(("ctx", "head"), None),
            P(("ctx", "head"), None),
            P(),
        ),
        out_specs=(P(("ctx", "head"), None), P(("ctx", "head"), None), P(("ctx", "head"), None)),
        check_vma=False,
    )
```

profile of v0, /device:TPU:8, one launch (start us, length us, event | category | flops | bytes accessed | tf_op | source)
XLA Modules:
  0.0 173.3 jit_solution(2294293589609892568)
XLA Ops:
  0.6 1.6 copy.114
  2.2 3.7 %all-to-all-start = ((bf16[64,4,256]{2,0,1:T(8,128)(2,1)}), bf16[64,4,256]{2,0,1:T(8,128)(2,1)S(1)}, u32[]{:S(2)}, u32[]{:S(2)}) async-start(bf16[64,4,256]{2,0,1:T(8,128)(2,1)} %bitcast.112), calls=%async_computation | async-start | bytes 262144 | tf_op jit(solution)/shard_map/all_to_all | solution.py:21
  5.9 1.6 copy.113
  7.5 3.5 %all-to-all-done = bf16[64,4,256]{2,0,1:T(8,128)(2,1)S(1)} async-done(((bf16[64,4,256]{2,0,1:T(8,128)(2,1)}), bf16[64,4,256]{2,0,1:T(8,128)(2,1)S(1)}, u32[]{:S(2)}, u32[]{:S(2)}) %all-to-all-start) | async-done | bytes 131104 | tf_op jit(solution)/shard_map/all_to_all | solution.py:21
  11.0 3.3 %all-to-all-start.1 = ((bf16[64,4,256]{2,0,1:T(8,128)(2,1)}), bf16[64,4,256]{2,0,1:T(8,128)(2,1)S(1)}, u32[]{:S(2)}, u32[]{:S(2)}) async-start(bf16[64,4,256]{2,0,1:T(8,128)(2,1)} %bitcast.111), calls=%async_computation.1 | async-start | bytes 262144 | tf_op jit(solution)/shard_map/all_to_all | solution.py:22
  14.3 2.3 %copy.112 = bf16[8,4,8,2048]{3,2,0,1:T(8,128)(2,1)} copy(bf16[8,4,8,2048]{3,2,1,0:T(8,128)(2,1)} %bitcast.128) | data formatting | bytes 2097152 | tf_op jit(solution)/shard_map/all_to_all | solution.py:20
  16.6 2.7 %all-to-all-done.1 = bf16[64,4,256]{2,0,1:T(8,128)(2,1)S(1)} async-done(((bf16[64,4,256]{2,0,1:T(8,128)(2,1)}), bf16[64,4,256]{2,0,1:T(8,128)(2,1)S(1)}, u32[]{:S(2)}, u32[]{:S(2)}) %all-to-all-start.1) | async-done | bytes 131104 | tf_op jit(solution)/shard_map/all_to_all | solution.py:22
  19.3 3.5 %all-to-all-start.2 = ((bf16[64,4,2048]{2,0,1:T(8,128)(2,1)}), bf16[64,4,2048]{2,0,1:T(8,128)(2,1)S(1)}, u32[]{:S(2)}, u32[]{:S(2)}) async-start(bf16[64,4,2048]{2,0,1:T(8,128)(2,1)} %bitcast.110), calls=%async_computation.2 | async-start | bytes 2097152 | tf_op jit(solution)/shard_map/all_to_all | solution.py:20
  22.8 1.9 %collective-permute-start = (bf16[2,256,256]{2,1,0:T(8,128)(2,1)S(1)}, bf16[2,256,256]{2,1,0:T(8,128)(2,1)S(1)}, u32[]{:S(2)}, u32[]{:S(2)}) collective-permute-start(bf16[2,256,256]{2,1,0:T(8,128)(2,1)S(1)} %pad_maximum_fusion.1), channel_id=1, source_target_pairs={{0,4},{4,8},{8,12},{12,16},{16,20},{20,24},{24,28},{1,5},{5,9},{9,... | collective-permute-start | bytes 786440 | tf_op jit(solution)/shard_map/ppermute | solution.py:12
  24.8 2.3 %copy.111 = bf16[8,4,8,2048]{3,2,0,1:T(8,128)(2,1)} copy(bf16[8,4,8,2048]{3,2,1,0:T(8,128)(2,1)} %bitcast.129) | data formatting | bytes 2097152 | tf_op jit(solution)/shard_map/all_to_all | solution.py:23
  27.1 7.0 %all-to-all-done.2 = bf16[64,4,2048]{2,0,1:T(8,128)(2,1)S(1)} async-done(((bf16[64,4,2048]{2,0,1:T(8,128)(2,1)}), bf16[64,4,2048]{2,0,1:T(8,128)(2,1)S(1)}, u32[]{:S(2)}, u32[]{:S(2)}) %all-to-all-start.2) | async-done | bytes 1048608 | tf_op jit(solution)/shard_map/all_to_all | solution.py:20
  34.1 3.5 %all-to-all-start.3 = ((bf16[64,4,2048]{2,0,1:T(8,128)(2,1)}), bf16[64,4,2048]{2,0,1:T(8,128)(2,1)S(1)}, u32[]{:S(2)}, u32[]{:S(2)}) async-start(bf16[64,4,2048]{2,0,1:T(8,128)(2,1)} %bitcast.109), calls=%async_computation.3 | async-start | bytes 2097152 | tf_op jit(solution)/shard_map/all_to_all | solution.py:23
  37.7 1.9 %collective-permute-start.1 = (bf16[2,256,256]{2,1,0:T(8,128)(2,1)S(1)}, bf16[2,256,256]{2,1,0:T(8,128)(2,1)}, u32[]{:S(2)}, u32[]{:S(2)}) collective-permute-start(bf16[2,256,256]{2,1,0:T(8,128)(2,1)S(1)} %collective-permute-done), channel_id=1, source_target_pairs={{0,4},{4,8},{8,12},{12,16},{16,20},{20,24},{24,28},{1,5},{5,9},{9,... | collective-permute-start | bytes 786440 | tf_op jit(solution)/shard_map/ppermute | solution.py:12
  39.7 5.7 %collective-permute-done.1 = bf16[2,256,256]{2,1,0:T(8,128)(2,1)} collective-permute-done((bf16[2,256,256]{2,1,0:T(8,128)(2,1)S(1)}, bf16[2,256,256]{2,1,0:T(8,128)(2,1)}, u32[]{:S(2)}, u32[]{:S(2)}) %collective-permute-start.1) | collective-permute-done | bytes 262176 | tf_op jit(solution)/shard_map/ppermute | solution.py:12
  45.4 1.9 %collective-permute-start.2 = (bf16[2,256,256]{2,1,0:T(8,128)(2,1)}, bf16[2,256,256]{2,1,0:T(8,128)(2,1)}, u32[]{:S(2)}, u32[]{:S(2)}) collective-permute-start(bf16[2,256,256]{2,1,0:T(8,128)(2,1)} %collective-permute-done.1), channel_id=1, source_target_pairs={{0,4},{4,8},{8,12},{12,16},{16,20},{20,24},{24,28},{1,5},{5,9},{9,... | collective-permute-start | bytes 786440 | tf_op jit(solution)/shard_map/ppermute | solution.py:12
  47.4 1.5 compare_and_fusion
  49.2 0.8 copy.77
  50.7 1.2 copy.106
  51.9 1.7 copy.71
  53.6 1.2 maximum_maximum_fusion
  54.8 1.0 fusion.20
  55.9 1.2 copy.67
  57.1 2.1 %copy.63 = bf16[1,1024,256]{1,2,0:T(8,128)(2,1)} copy(bf16[1,1024,256]{2,1,0:T(8,128)(2,1)} %get-tuple-element.4) | data formatting | bytes 1048576 | tf_op jit(solution)/shard_map/slice | solution.py:34
  59.2 9.6 %fusion.23 = (f32[2,8,256]{2,1,0:T(8,128)S(1)}, f32[2,8,256,1024]{2,3,1,0:T(8,128)}) fusion(pred[256,1024]{0,1:T(8,128)(4,1)S(1)} %copy-done.3, bf16[1024,2,128,1]{0,2,3,1:T(8,128)(2,1)} %bitcast.122, bf16[256,2,8,128]{0,3,2,1:T(8,128)(2,1)S(1)} %copy.77), kind=kOutput, calls=%fused_computation.48 | convolution fusion | flops 1090520064 | bytes 18628608 | tf_op jit(solution)/shard_map/sub | solution.py:60
  68.8 6.6 %fusion.7 = bf16[2,8,256,1024]{2,3,1,0:T(8,128)(2,1)S(1)} fusion(f32[2,8,256,1024]{2,3,1,0:T(8,128)} %get-tuple-element.13, f32[2,8,256]{2,1,0:T(8,128)S(1)} %get-tuple-element.12), kind=kLoop, calls=%fused_computation.11 | loop fusion | flops 8388608 | bytes 25182208 | tf_op jit(solution)/shard_map/convert_element_type | solution.py:62
  75.4 3.8 %fusion.24 = f32[2,1024,128,1]{1,2,3,0:T(8,128)} fusion(bf16[2,8,256,1024]{2,3,1,0:T(8,128)(2,1)S(1)} %fusion.7, bf16[256,2,8,128]{0,3,2,1:T(8,128)(2,1)S(1)} %copy.71), kind=kOutput, calls=%fused_computation.49 | convolution fusion | flops 1073741824 | bytes 10485760 | tf_op jit(solution)/shard_map/kgij,ikgd->jkd/dot_general | solution.py:68
  79.2 1.3 fusion.8
  80.5 1.6 copy.81
  82.1 7.1 %fusion.2 = bf16[2,8,256,1024]{2,3,1,0:T(8,128)(2,1)S(1)} fusion(f32[2,8,256]{2,1,0:T(8,128)S(1)} %bitcast.137, f32[2,8,256,1024]{2,3,1,0:T(8,128)} %get-tuple-element.13, f32[2,8,256]{2,1,0:T(8,128)S(1)} %get-tuple-element.12, bf16[1024,2,128,1]{0,2,3,1:T(8,128)(2,1)S(1)} %bitcast.120, bf16[256,2,8,128]{0,3,2,1:T(8,128)(2,1)S(1)} %copy.71), kind=kOutput, calls=%fused_computation.3 | convolution fusion | flops 1090519040 | bytes 26771456 | tf_op jit(solution)/shard_map/ikgd,jkd->kgij/dot_general | solution.py:71
  89.2 3.2 %copy-done = bf16[2,8,256,1024]{2,3,1,0:T(8,128)(2,1)} copy-done((bf16[2,8,256,1024]{2,3,1,0:T(8,128)(2,1)}, bf16[2,8,256,1024]{2,3,1,0:T(8,128)(2,1)S(1)}, u32[]{:S(2)}) %copy-start) | copy-done | bytes 8388632
  92.5 5.1 %fusion.11 = f32[2,1024,128]{1,2,0:T(8,128)} fusion(bf16[2,8,256,1024]{2,3,1,0:T(8,128)(2,1)S(1)} %fusion.2, bf16[256,2,8,128]{0,3,2,1:T(8,128)(2,1)} %copy-done.1), kind=kOutput, calls=%fused_computation.23 | convolution fusion | flops 1074003968 | bytes 10485760 | tf_op jit(solution)/shard_map/kgij,ikgd->jkd/dot_general | solution.py:80
  97.6 1.6 copy.80
  99.2 3.0 %collective-permute-start.3 = (f32[2,256,256]{2,1,0:T(8,128)S(1)}, f32[2,256,256]{2,1,0:T(8,128)S(1)}, u32[]{:S(2)}, u32[]{:S(2)}) collective-permute-start(f32[2,256,256]{2,1,0:T(8,128)S(1)} %fusion.14), channel_id=1, source_target_pairs={{4,0},{8,4},{12,8},{16,12},{20,16},{24,20},{28,24},{5,1},{9,5},{13... | collective-permute-start | bytes 1572872 | tf_op jit(solution)/shard_map/ppermute | solution.py:12
  102.1 6.7 %collective-permute-done.3 = f32[2,256,256]{2,1,0:T(8,128)S(1)} collective-permute-done((f32[2,256,256]{2,1,0:T(8,128)S(1)}, f32[2,256,256]{2,1,0:T(8,128)S(1)}, u32[]{:S(2)}, u32[]{:S(2)}) %collective-permute-start.3) | collective-permute-done | bytes 524320 | tf_op jit(solution)/shard_map/ppermute | solution.py:12
  108.8 0.9 fusion.16
  109.8 4.0 %collective-permute-start.4 = (f32[2,256,256]{2,1,0:T(8,128)}, f32[2,256,256]{2,1,0:T(8,128)}, u32[]{:S(2)}, u32[]{:S(2)}) collective-permute-start(f32[2,256,256]{2,1,0:T(8,128)} %fusion.16), channel_id=1, source_target_pairs={{4,0},{8,4},{12,8},{16,12},{20,16},{24,20},{28,24},{5,1},{9,5},{13... | collective-permute-start | bytes 1572872 | tf_op jit(solution)/shard_map/ppermute | solution.py:12
  113.8 6.0 %multiply_bitcast_fusion = f32[256,2,8,128]{0,3,2,1:T(8,128)} fusion(bf16[1024,2,128,1]{0,2,3,1:T(8,128)(2,1)S(1)} %bitcast.123, bf16[2,8,256,1024]{2,3,1,0:T(8,128)(2,1)} %copy-done), kind=kOutput, calls=%fused_computation.20 | convolution fusion | flops 1074266112 | bytes 11010048 | tf_op jit(solution)/shard_map/kgij,jkd->ikgd/dot_general | solution.py:76
  119.8 3.0 %copy.74 = f32[256,2,8,128]{3,2,1,0:T(8,128)} copy(f32[256,2,8,128]{0,3,2,1:T(8,128)} %multiply_bitcast_fusion) | data formatting | bytes 4194304 | tf_op jit(solution)/shard_map/mul | solution.py:76
  122.8 2.7 %all_to_all.102 = f32[4,64,2048]{2,1,0:T(8,128)} reshape(f32[256,2,8,128]{3,2,1,0:T(8,128)} %copy.74) | data formatting | bytes 4194304 | tf_op jit(solution)/shard_map/all_to_all | solution.py:93
  125.5 4.5 %all-to-all-start.4 = ((f32[4,64,2048]{2,1,0:T(8,128)}), f32[4,64,2048]{2,1,0:T(8,128)}, u32[]{:S(2)}, u32[]{:S(2)}) async-start(f32[4,64,2048]{2,1,0:T(8,128)} %all_to_all.102), calls=%async_computation.4 | async-start | bytes 4194304 | tf_op jit(solution)/shard_map/all_to_all | solution.py:93
  130.0 1.1 fusion.13
  131.1 1.9 %collective-permute-start.5 = (f32[2,256,256]{2,1,0:T(8,128)S(1)}, f32[2,256,256]{2,1,0:T(8,128)S(1)}, u32[]{:S(2)}, u32[]{:S(2)}) collective-permute-start(f32[2,256,256]{2,1,0:T(8,128)S(1)} %fusion.13), channel_id=1, source_target_pairs={{4,0},{8,4},{12,8},{16,12},{20,16},{24,20},{28,24},{5,1},{9,5},{13... | collective-permute-start | bytes 1572872 | tf_op jit(solution)/shard_map/ppermute | solution.py:12
  133.0 6.7 %collective-permute-done.5 = f32[2,256,256]{2,1,0:T(8,128)S(1)} collective-permute-done((f32[2,256,256]{2,1,0:T(8,128)S(1)}, f32[2,256,256]{2,1,0:T(8,128)S(1)}, u32[]{:S(2)}, u32[]{:S(2)}) %collective-permute-start.5) | collective-permute-done | bytes 524320 | tf_op jit(solution)/shard_map/ppermute | solution.py:12
  140.5 15.0 %all-to-all-done.4 = f32[4,64,2048]{2,1,0:T(8,128)} async-done(((f32[4,64,2048]{2,1,0:T(8,128)}), f32[4,64,2048]{2,1,0:T(8,128)}, u32[]{:S(2)}, u32[]{:S(2)}) %all-to-all-start.4) | async-done | bytes 2097184 | tf_op jit(solution)/shard_map/all_to_all | solution.py:93
  155.5 8.3 %all_to_all.121 = f32[4,64,256]{2,1,0:T(8,128)S(1)} all-to-all(f32[4,64,256]{2,1,0:T(8,128)S(1)} %bitcast.132), channel_id=1, replica_groups=mesh['ctx'=8,'head'=4] {'head'}, dimensions={0} | all-to-all | bytes 524288 | tf_op jit(solution)/shard_map/all_to_all | solution.py:94
  163.8 3.4 %all-to-all-start.6 = ((f32[4,64,256]{2,1,0:T(8,128)}), f32[4,64,256]{2,1,0:T(8,128)S(1)}, u32[]{:S(2)}, u32[]{:S(2)}) async-start(f32[4,64,256]{2,1,0:T(8,128)} %bitcast.30), calls=%async_computation.6 | async-start | bytes 524288 | tf_op jit(solution)/shard_map/all_to_all | solution.py:95
  167.2 3.1 %copy.102 = f32[4,8,8,2048]{3,2,0,1:T(8,128)} copy(f32[4,8,8,2048]{3,2,1,0:T(8,128)} %bitcast.53) | data formatting | bytes 4194304 | tf_op jit(solution)/shard_map/all_to_all | solution.py:93
  171.1 1.5 all-to-all-done.6
  (26 shorter events, 3.5 us)
Async XLA Ops:
  0.6 39.0 %copy-start.5 = (s32[2048]{0:T(1024)S(1)}, s32[2048]{0:T(1024)}, u32[]{:S(2)}) copy-start(s32[2048]{0:T(1024)} %param.9) | copy-start | bytes 24580
  2.2 8.7 %all-to-all-start = ((bf16[64,4,256]{2,0,1:T(8,128)(2,1)}), bf16[64,4,256]{2,0,1:T(8,128)(2,1)S(1)}, u32[]{:S(2)}, u32[]{:S(2)}) async-start(bf16[64,4,256]{2,0,1:T(8,128)(2,1)} %bitcast.112), calls=%async_computation | async-start | bytes 262144 | tf_op jit(solution)/shard_map/all_to_all | solution.py:21
  11.0 8.3 %all-to-all-start.1 = ((bf16[64,4,256]{2,0,1:T(8,128)(2,1)}), bf16[64,4,256]{2,0,1:T(8,128)(2,1)S(1)}, u32[]{:S(2)}, u32[]{:S(2)}) async-start(bf16[64,4,256]{2,0,1:T(8,128)(2,1)} %bitcast.111), calls=%async_computation.1 | async-start | bytes 262144 | tf_op jit(solution)/shard_map/all_to_all | solution.py:22
  19.3 14.8 %all-to-all-start.2 = ((bf16[64,4,2048]{2,0,1:T(8,128)(2,1)}), bf16[64,4,2048]{2,0,1:T(8,128)(2,1)S(1)}, u32[]{:S(2)}, u32[]{:S(2)}) async-start(bf16[64,4,2048]{2,0,1:T(8,128)(2,1)} %bitcast.110), calls=%async_computation.2 | async-start | bytes 2097152 | tf_op jit(solution)/shard_map/all_to_all | solution.py:20
  22.8 14.8 %collective-permute-start = (bf16[2,256,256]{2,1,0:T(8,128)(2,1)S(1)}, bf16[2,256,256]{2,1,0:T(8,128)(2,1)S(1)}, u32[]{:S(2)}, u32[]{:S(2)}) collective-permute-start(bf16[2,256,256]{2,1,0:T(8,128)(2,1)S(1)} %pad_maximum_fusion.1), channel_id=1, source_target_pairs={{0,4},{4,8},{8,12},{12,16},{16,20},{20,24},{24,28},{1,5},{5,9},{9,... | collective-permute-start | bytes 786440 | tf_op jit(solution)/shard_map/ppermute | solution.py:12
  34.1 16.6 %all-to-all-start.3 = ((bf16[64,4,2048]{2,0,1:T(8,128)(2,1)}), bf16[64,4,2048]{2,0,1:T(8,128)(2,1)S(1)}, u32[]{:S(2)}, u32[]{:S(2)}) async-start(bf16[64,4,2048]{2,0,1:T(8,128)(2,1)} %bitcast.109), calls=%async_computation.3 | async-start | bytes 2097152 | tf_op jit(solution)/shard_map/all_to_all | solution.py:23
  37.6 11.3 %copy-start.4 = (bf16[2,256,256]{2,1,0:T(8,128)(2,1)}, bf16[2,256,256]{2,1,0:T(8,128)(2,1)S(1)}, u32[]{:S(2)}) copy-start(bf16[2,256,256]{2,1,0:T(8,128)(2,1)S(1)} %collective-permute-done) | copy-start | bytes 786436
  37.7 7.8 %collective-permute-start.1 = (bf16[2,256,256]{2,1,0:T(8,128)(2,1)S(1)}, bf16[2,256,256]{2,1,0:T(8,128)(2,1)}, u32[]{:S(2)}, u32[]{:S(2)}) collective-permute-start(bf16[2,256,256]{2,1,0:T(8,128)(2,1)S(1)} %collective-permute-done), channel_id=1, source_target_pairs={{0,4},{4,8},{8,12},{12,16},{16,20},{20,24},{24,28},{1,5},{5,9},{9,... | collective-permute-start | bytes 786440 | tf_op jit(solution)/shard_map/ppermute | solution.py:12
  45.4 8.2 %collective-permute-start.2 = (bf16[2,256,256]{2,1,0:T(8,128)(2,1)}, bf16[2,256,256]{2,1,0:T(8,128)(2,1)}, u32[]{:S(2)}, u32[]{:S(2)}) collective-permute-start(bf16[2,256,256]{2,1,0:T(8,128)(2,1)} %collective-permute-done.1), channel_id=1, source_target_pairs={{0,4},{4,8},{8,12},{12,16},{16,20},{20,24},{24,28},{1,5},{5,9},{9,... | collective-permute-start | bytes 786440 | tf_op jit(solution)/shard_map/ppermute | solution.py:12
  50.0 18.8 %copy-start.1 = (bf16[256,2,8,128]{0,3,2,1:T(8,128)(2,1)}, bf16[256,2,8,128]{0,3,2,1:T(8,128)(2,1)S(1)}, u32[]{:S(2)}) copy-start(bf16[256,2,8,128]{0,3,2,1:T(8,128)(2,1)S(1)} %copy.77) | copy-start | bytes 3145732
  51.9 7.2 %copy-start.3 = (pred[256,1024]{0,1:T(8,128)(4,1)S(1)}, pred[256,1024]{0,1:T(8,128)(4,1)}, u32[]{:S(2)}) copy-start(pred[256,1024]{0,1:T(8,128)(4,1)} %compare_and_fusion) | copy-start | bytes 786436
  89.2 3.2 %copy-start = (bf16[2,8,256,1024]{2,3,1,0:T(8,128)(2,1)}, bf16[2,8,256,1024]{2,3,1,0:T(8,128)(2,1)S(1)}, u32[]{:S(2)}) copy-start(bf16[2,8,256,1024]{2,3,1,0:T(8,128)(2,1)S(1)} %fusion.2) | copy-start | bytes 25165828
  92.5 21.3 %copy-start.2 = (bf16[1,1024,256]{1,2,0:T(8,128)(2,1)S(1)}, bf16[1,1024,256]{1,2,0:T(8,128)(2,1)}, u32[]{:S(2)}) copy-start(bf16[1,1024,256]{1,2,0:T(8,128)(2,1)} %copy.63) | copy-start | bytes 1572868
  99.2 9.7 %collective-permute-start.3 = (f32[2,256,256]{2,1,0:T(8,128)S(1)}, f32[2,256,256]{2,1,0:T(8,128)S(1)}, u32[]{:S(2)}, u32[]{:S(2)}) collective-permute-start(f32[2,256,256]{2,1,0:T(8,128)S(1)} %fusion.14), channel_id=1, source_target_pairs={{4,0},{8,4},{12,8},{16,12},{20,16},{24,20},{28,24},{5,1},{9,5},{13... | collective-permute-start | bytes 1572872 | tf_op jit(solution)/shard_map/ppermute | solution.py:12
  109.8 20.2 %collective-permute-start.4 = (f32[2,256,256]{2,1,0:T(8,128)}, f32[2,256,256]{2,1,0:T(8,128)}, u32[]{:S(2)}, u32[]{:S(2)}) collective-permute-start(f32[2,256,256]{2,1,0:T(8,128)} %fusion.16), channel_id=1, source_target_pairs={{4,0},{8,4},{12,8},{16,12},{20,16},{24,20},{28,24},{5,1},{9,5},{13... | collective-permute-start | bytes 1572872 | tf_op jit(solution)/shard_map/ppermute | solution.py:12
  125.5 30.0 %all-to-all-start.4 = ((f32[4,64,2048]{2,1,0:T(8,128)}), f32[4,64,2048]{2,1,0:T(8,128)}, u32[]{:S(2)}, u32[]{:S(2)}) async-start(f32[4,64,2048]{2,1,0:T(8,128)} %all_to_all.102), calls=%async_computation.4 | async-start | bytes 4194304 | tf_op jit(solution)/shard_map/all_to_all | solution.py:93
  131.1 8.6 %collective-permute-start.5 = (f32[2,256,256]{2,1,0:T(8,128)S(1)}, f32[2,256,256]{2,1,0:T(8,128)S(1)}, u32[]{:S(2)}, u32[]{:S(2)}) collective-permute-start(f32[2,256,256]{2,1,0:T(8,128)S(1)} %fusion.13), channel_id=1, source_target_pairs={{4,0},{8,4},{12,8},{16,12},{20,16},{24,20},{28,24},{5,1},{9,5},{13... | collective-permute-start | bytes 1572872 | tf_op jit(solution)/shard_map/ppermute | solution.py:12
  163.8 8.8 %all-to-all-start.6 = ((f32[4,64,256]{2,1,0:T(8,128)}), f32[4,64,256]{2,1,0:T(8,128)S(1)}, u32[]{:S(2)}, u32[]{:S(2)}) async-start(f32[4,64,256]{2,1,0:T(8,128)} %bitcast.30), calls=%async_computation.6 | async-start | bytes 524288 | tf_op jit(solution)/shard_map/all_to_all | solution.py:95
where the time goes:
time: 175 us; the launch traced here: 173 us
  waiting for transfers between devices  49.4 us (28%)
  starting transfers between devices  36.6 us (21%)
  local copies, waits for them, and re-layouts  33.5 us (19%)
  matrix products  32.9 us (19%)
  other arithmetic  11.6 us (7%)
  blocking collectives  8.28 us (5%)
    ppermute x6, waiting for transfers between devices, passed_along(): return lax.ppermute(array, axis, pairs)  19.1 us
    all_to_all x1, waiting for transfers between devices, body(): lax.all_to_all(query_rows, 'head', split_axis=0, concat_axis=1, tiled=True)  15 us
    ppermute x6, starting transfers between devices, passed_along(): return lax.ppermute(array, axis, pairs)  14.6 us
    sub x1, matrix products, body(): expo = jnp.exp(scores - row_max)  9.64 us
    all_to_all x1, blocking collectives, body(): lax.all_to_all(total[0], 'head', split_axis=0, concat_axis=1, tiled=True)  8.28 us
    dot_general x1, matrix products, body(): jnp.einsum('ikgd,jkd->kgij', grad_heads, value_win, preferred_element_typ...  7.12 us
    all_to_all x1, waiting for transfers between devices, body(): lax.all_to_all(queries, 'head', split_axis=1, concat_axis=0, tiled=True)  7.03 us
    convert_element_type x1, other arithmetic, body(): weight_bf = weights.astype(jnp.bfloat16)  6.62 us
  transfers between devices with their start and end apart: 12, of which 9 were waited for; matrix products, arithmetic and copies ran while one was open for 15% of the time, Pallas kernels for 0%

commit v1 on v0

v1 whole, which is shorter than its diff:
```python
import functools
import math
import jax
import jax.numpy as jnp
from jax import lax
from jax.experimental import pallas as pl
from jax.experimental.pallas import tpu as pltpu
from jax.sharding import PartitionSpec as P

HD = 128
BACK = 3
CHUNK = 2
MESH = pl.DeviceIdType.MESH
NT = (((1,), (1,)), ((), ()))


def kernel(
    n_ctx, n_head, group,
    q_ref, k_ref, v_ref, g_ref, doc_ref,
    dq_out, dk_out, dv_out,
    q_buf, g_buf, dq_buf, kv_buf, kt_buf, acc, bias, part_out, part_in, own_part, tot,
    own_sem, kv_send, kv_recv, ctx_send, ctx_recv, in_send, in_recv,
    dq_send, dq_recv, part_send, part_recv, tot_send, tot_recv,
):
    c = lax.axis_index("ctx")
    h = lax.axis_index("head")
    rows = q_ref.shape[0]
    blk = rows * n_head
    kv_n = kv_buf.shape[0]
    n_chunk, _, width = q_buf.shape
    per_kv = n_chunk // kv_n
    cols = n_chunk * width
    scale = 1.0 / HD**0.5
    spread = range(1, BACK + 1)

    def peer(p):
        other, bit = 0, 1
        while bit < n_head:
            other = other + ((h // bit) % 2 + (p // bit) % 2) % 2 * bit
            bit *= 2
        return other

    barrier = pltpu.get_barrier_semaphore()
    for p in range(1, n_head):
        pl.semaphore_signal(barrier, inc=1, device_id=(c, peer(p)), device_id_type=MESH)
    for s in spread:
        for to in ((c + s) % n_ctx, (c - s + n_ctx) % n_ctx):
            pl.semaphore_signal(barrier, inc=1, device_id=(to, h), device_id_type=MESH)
    pl.semaphore_wait(barrier, n_head - 1 + 2 * BACK)

    def at(n, size):
        return pl.ds(pl.multiple_of(n * size, size), size)

    def kv_copy(kv, t, p):
        to = peer(p)
        ref = (k_ref, v_ref)[t]
        return pltpu.make_async_remote_copy(
            src_ref=ref.at[:, at(to * kv_n + kv, HD)],
            dst_ref=kv_buf.at[kv, BACK, t, at(h, rows)],
            send_sem=kv_send.at[kv, t, p - 1],
            recv_sem=kv_recv.at[kv, t, p - 1],
            device_id=(c, to), device_id_type=MESH,
        )

    def kv_own(kv, t):
        ref = (k_ref, v_ref)[t]
        return pltpu.make_async_copy(
            ref.at[:, at(h * kv_n + kv, HD)], kv_buf.at[kv, BACK, t, at(h, rows)],
            own_sem.at[kv, t],
        )

    def in_copy(ch, t, p):
        to = peer(p)
        return pltpu.make_async_remote_copy(
            src_ref=(q_ref, g_ref)[t].at[:, at(to * n_chunk + ch, width)],
            dst_ref=(q_buf, g_buf)[t].at[ch, at(h, rows)],
            send_sem=in_send.at[ch, t, p - 1],
            recv_sem=in_recv.at[ch, t, p - 1],
            device_id=(c, to), device_id_type=MESH,
        )

    def in_own(ch, t):
        return pltpu.make_async_copy(
            (q_ref, g_ref)[t].at[:, at(h * n_chunk + ch, width)],
            (q_buf, g_buf)[t].at[ch, at(h, rows)],
            in_recv.at[ch, t, n_head - 1],
        )

    def ctx_copy(kv, s):
        return pltpu.make_async_remote_copy(
            src_ref=kv_buf.at[kv, BACK], dst_ref=kv_buf.at[kv, BACK - s],
            send_sem=ctx_send.at[kv, s - 1], recv_sem=ctx_recv.at[kv, s - 1],
            device_id=((c + s) % n_ctx, h), device_id_type=MESH,
        )

    def dq_copy(ch, p):
        to = peer(p)
        return pltpu.make_async_remote_copy(
            src_ref=dq_buf.at[ch, at(to, rows)],
            dst_ref=dq_out.at[:, at(h * n_chunk + ch, width)],
            send_sem=dq_send.at[ch, p - 1], recv_sem=dq_recv.at[ch, p - 1],
            device_id=(c, to), device_id_type=MESH,
        )

    def dq_own(ch):
        return pltpu.make_async_copy(
            dq_buf.at[ch, at(h, rows)], dq_out.at[:, at(h * n_chunk + ch, width)],
            dq_send.at[ch, n_head - 1],
        )

    def part_copy(kv, s):
        return pltpu.make_async_remote_copy(
            src_ref=part_out.at[kv, s - 1], dst_ref=part_in.at[kv, s - 1],
            send_sem=part_send.at[kv, s - 1], recv_sem=part_recv.at[kv, s - 1],
            device_id=((c - s + n_ctx) % n_ctx, h), device_id_type=MESH,
        )

    def tot_copy(kv, t, p):
        to = peer(p)
        return pltpu.make_async_remote_copy(
            src_ref=tot.at[kv, t, at(to, rows)],
            dst_ref=(dk_out, dv_out)[t].at[:, at(h * kv_n + kv, HD)],
            send_sem=tot_send.at[kv, t, p - 1], recv_sem=tot_recv.at[kv, t, p - 1],
            device_id=(c, to), device_id_type=MESH,
        )

    def tot_own(kv, t):
        return pltpu.make_async_copy(
            tot.at[kv, t, at(h, rows)], (dk_out, dv_out)[t].at[:, at(h * kv_n + kv, HD)],
            tot_send.at[kv, t, n_head - 1],
        )

    others = range(1, n_head)
    for kv in range(kv_n):
        for t in range(2):
            for p in others:
                kv_copy(kv, t, p).start()
            kv_own(kv, t).start()

    @pl.loop(0, n_chunk)
    def _(ch):
        for t in range(2):
            for p in others:
                in_copy(ch, t, p).start()
            in_own(ch, t).start()

    for kv in range(kv_n):
        for t in range(2):
            kv_own(kv, t).wait()
            for p in others:
                kv_copy(kv, t, p).wait_recv()
        for s in spread:
            @pl.when(c + s < n_ctx)
            def _():
                ctx_copy(kv, s).start()

            @pl.when(c < s)
            def _():
                kv_buf[kv, BACK - s] = jnp.zeros(kv_buf.shape[2:], kv_buf.dtype)

    tile = HD
    query_doc = doc_ref[:, pl.ds(pl.multiple_of(c * blk, blk), blk)].astype(jnp.float32)
    for part in range(4 * blk // tile):
        key_blk = jnp.maximum(c - BACK + part * tile // blk, 0)
        start = pl.multiple_of(key_blk * blk + part * tile % blk, tile)
        key_row = doc_ref[:, pl.ds(start, tile)].astype(jnp.float32)
        key_doc = jnp.transpose(jnp.broadcast_to(key_row, (tile, tile)))
        key_doc = jnp.concatenate([key_doc] * (blk // tile), axis=1)
        j = lax.broadcasted_iota(jnp.int32, (tile, blk), 0) + part * tile
        i = lax.broadcasted_iota(jnp.int32, (tile, blk), 1)
        ok = (j > i) & (j <= i + BACK * blk) & (j + (c - BACK) * blk >= 0)
        ok = ok & (key_doc == query_doc)
        bias[pl.ds(part * tile, tile)] = jnp.where(ok, 0.0, -1e30)

    for kv in range(kv_n):
        for s in spread:
            @pl.when(c >= s)
            def _():
                ctx_copy(kv, s).wait_recv()

        keys = kv_buf[kv, :, 0].reshape(4 * blk, HD)
        kt_buf[...] = jnp.transpose(keys.astype(jnp.float32)).astype(jnp.bfloat16)
        acc[...] = jnp.zeros(acc.shape, acc.dtype)

        @pl.loop(0, per_kv)
        def _(step):
            ch = kv * per_kv + step
            for t in range(2):
                in_own(ch, t).wait()
                for p in others:
                    in_copy(ch, t, p).wait_recv()
            for a in range(width // HD):
                lanes = pl.ds(a * HD, HD)
                q = q_buf[ch, :, lanes]
                g = g_buf[ch, :, lanes]
                key_win = kv_buf[kv, :, 0].reshape(4 * blk, HD)
                val_win = kv_buf[kv, :, 1].reshape(4 * blk, HD)
                s_t = lax.dot_general(key_win, q, NT, preferred_element_type=jnp.float32)
                s_t = s_t + bias[...]
                top = jnp.max(s_t, axis=0, keepdims=True)
                e_t = jnp.exp2((s_t - top) * (scale * math.log2(math.e)))
                w_t = e_t * (1.0 / jnp.sum(e_t, axis=0, keepdims=True))
                w_bf = w_t.astype(jnp.bfloat16)
                p_t = lax.dot_general(val_win, g, NT, preferred_element_type=jnp.float32)
                delta = jnp.sum(w_bf.astype(jnp.float32) * p_t, axis=0, keepdims=True)
                d_t = (w_t * (p_t - delta)).astype(jnp.bfloat16)
                dv = jnp.dot(w_bf, g, preferred_element_type=jnp.float32)
                dk = jnp.dot(d_t, q, preferred_element_type=jnp.float32)
                acc[:, 0] += dk.reshape(4, blk, HD)
                acc[:, 1] += dv.reshape(4, blk, HD)
                dq_t = jnp.dot(kt_buf[...], d_t, preferred_element_type=jnp.float32)
                dq_buf[ch, :, lanes] = jnp.transpose(dq_t * scale).astype(jnp.bfloat16)
            for p in others:
                dq_copy(ch, p).start()
            dq_own(ch).start()

        for s in spread:
            part_out[kv, s - 1, 0] = (acc[BACK - s, 0] * scale).astype(jnp.bfloat16)
            part_out[kv, s - 1, 1] = acc[BACK - s, 1].astype(jnp.bfloat16)

            @pl.when(c >= s)
            def _():
                part_copy(kv, s).start()
        own_part[kv, 0] = acc[BACK, 0] * scale
        own_part[kv, 1] = acc[BACK, 1]

    for kv in range(kv_n):
        for s in spread:
            @pl.when(c + s < n_ctx)
            def _():
                part_copy(kv, s).wait_recv()
                own_part[kv] += part_in[kv, s - 1].astype(jnp.float32)

        tot[kv] = own_part[kv].astype(jnp.bfloat16)
        for t in range(2):
            for p in others:
                tot_copy(kv, t, p).start()
            tot_own(kv, t).start()

    @pl.loop(0, n_chunk)
    def _(ch):
        for t in range(2):
            for p in others:
                in_copy(ch, t, p).wait_send()
        for p in others:
            dq_copy(ch, p).wait()
        dq_own(ch).wait()

    for kv in range(kv_n):
        for t in range(2):
            for p in others:
                kv_copy(kv, t, p).wait_send()
                tot_copy(kv, t, p).wait()
            tot_own(kv, t).wait()
        for s in spread:
            @pl.when(c + s < n_ctx)
            def _():
                ctx_copy(kv, s).wait_send()

            @pl.when(c >= s)
            def _():
                part_copy(kv, s).wait_send()


def body(queries, keys, values, out_grad, doc_ids):
    n_ctx, n_head = lax.axis_size("ctx"), lax.axis_size("head")
    rows, q_cols = queries.shape
    kv_cols = keys.shape[1]
    blk = rows * n_head
    kv_n = kv_cols // HD // n_head
    group = q_cols // kv_cols
    chunk = math.gcd(CHUNK, group)
    width = chunk * HD
    n_chunk = kv_n * group // chunk
    win = BACK + 1
    bf, f32, dma = jnp.bfloat16, jnp.float32, pltpu.SemaphoreType.DMA
    far = pl.BlockSpec(memory_space=pl.ANY)
    near = pl.BlockSpec(memory_space=pltpu.VMEM)
    dq, dk, dv = pl.pallas_call(
        functools.partial(kernel, n_ctx, n_head, group),
        out_shape=(
            jax.ShapeDtypeStruct((rows, q_cols), bf),
            jax.ShapeDtypeStruct((rows, kv_cols), bf),
            jax.ShapeDtypeStruct((rows, kv_cols), bf),
        ),
        in_specs=[far, far, far, far, near],
        out_specs=(far, far, far),
        scratch_shapes=[
            pltpu.VMEM((n_chunk, blk, width), bf),
            pltpu.VMEM((n_chunk, blk, width), bf),
            pltpu.VMEM((n_chunk, blk, width), bf),
            pltpu.VMEM((kv_n, win, 2, blk, HD), bf),
            pltpu.VMEM((HD, win * blk), bf),
            pltpu.VMEM((win, 2, blk, HD), f32),
            pltpu.VMEM((win * blk, blk), f32),
            pltpu.VMEM((kv_n, BACK, 2, blk, HD), bf),
            pltpu.VMEM((kv_n, BACK, 2, blk, HD), bf),
            pltpu.VMEM((kv_n, 2, blk, HD), f32),
            pltpu.VMEM((kv_n, 2, blk, HD), bf),
            dma((kv_n, 2)),
            dma((kv_n, 2, n_head)),
            dma((kv_n, 2, n_head)),
            dma((kv_n, BACK)),
            dma((kv_n, BACK)),
            dma((n_chunk, 2, n_head)),
            dma((n_chunk, 2, n_head)),
            dma((n_chunk, n_head)),
            dma((n_chunk, n_head)),
            dma((kv_n, BACK)),
            dma((kv_n, BACK)),
            dma((kv_n, 2, n_head)),
            dma((kv_n, 2, n_head)),
        ],
        compiler_params=pltpu.CompilerParams(
            collective_id=0, has_side_effects=True, vmem_limit_bytes=56 * 2**20
        ),
    )(queries, keys, values, out_grad, doc_ids.reshape(1, -1))
    return dq.astype(f32), dk.astype(f32), dv.astype(f32)


def solution(mesh):
    split = P(("ctx", "head"), None)
    return jax.shard_map(
        body,
        mesh=mesh,
        in_specs=(split, split, split, split, P()),
        out_specs=(split, split, split),
        check_vma=False,
    )
```

time: 175 us -> 62.1 us (0.35)
  the two profiles are of different devices: /device:TPU:8 before, /device:TPU:1 now
where the time goes in v1:
time: 62.1 us; the launch traced here: 61.9 us
  Pallas kernels  57 us (92%)
  other arithmetic  4.16 us (7%)
  between operations  0.66 us (1%)
    pallas_call x1, Pallas kernels, body(): pl.pallas_call(functools.partial(kernel, n_ctx, n_head, group), out_shape...  57 us
    convert_element_type x3, other arithmetic, body(): return (dq.astype(f32), dk.astype(f32), dv.astype(f32))  4.16 us

profile of v1, /device:TPU:1, one launch (start us, length us, event | category | flops | bytes accessed | tf_op | source)
XLA Modules:
  0.0 61.9 jit_solution(14135818594508323889)
XLA Ops:
  0.6 57.0 %shard_map.76 = (bf16[64,8192]{1,0:T(8,128)(2,1)}, bf16[64,1024]{1,0:T(8,128)(2,1)}, bf16[64,1024]{1,0:T(8,128)(2,1)}) custom-call(bf16[64,8192]{1,0:T(8,128)(2,1)} %q_ref.1, bf16[64,1024]{1,0:T(8,128)(2,1)} %k_ref.1, bf16[64,1024]{1,0:T(8,128)(2,1)} %v_ref.1, bf16[64,8192]{1,0:T(8,128)(2,1)} %g_ref.1, s32[1,2048]{1,0:T(1,128)} %bitcast.1), custom_call_target="tpu_custom_call" | custom-call | tf_op jit(solution)/shard_map/pallas_call | solution.py:279
  57.7 0.0 copy-start.1
  57.7 0.0 copy-start
  57.7 2.7 %convert_element_type.9 = f32[64,8192]{1,0:T(8,128)} convert(bf16[64,8192]{1,0:T(8,128)(2,1)} %get-tuple-element.6) | non-fusion elementwise | flops 524288 | bytes 3145728 | tf_op jit(solution)/shard_map/convert_element_type | solution.py:318
  60.4 0.0 copy-done.1
  60.4 0.7 %convert_element_type.10 = f32[64,1024]{1,0:T(8,128)} convert(bf16[64,1024]{1,0:T(8,128)(2,1)S(1)} %copy-done.1) | non-fusion elementwise | flops 65536 | bytes 393216 | tf_op jit(solution)/shard_map/convert_element_type | solution.py:318
  61.1 0.0 copy-done
  61.2 0.7 %convert_element_type.11 = f32[64,1024]{1,0:T(8,128)} convert(bf16[64,1024]{1,0:T(8,128)(2,1)S(1)} %copy-done) | non-fusion elementwise | flops 65536 | bytes 393216 | tf_op jit(solution)/shard_map/convert_element_type | solution.py:318
Async XLA Ops:
  57.7 2.7 %copy-start.1 = (bf16[64,1024]{1,0:T(8,128)(2,1)S(1)}, bf16[64,1024]{1,0:T(8,128)(2,1)}, u32[]{:S(2)}) copy-start(bf16[64,1024]{1,0:T(8,128)(2,1)} %get-tuple-element.7) | copy-start | bytes 393220
  57.7 3.5 %copy-start = (bf16[64,1024]{1,0:T(8,128)(2,1)S(1)}, bf16[64,1024]{1,0:T(8,128)(2,1)}, u32[]{:S(2)}) copy-start(bf16[64,1024]{1,0:T(8,128)(2,1)} %get-tuple-element.8) | copy-start | bytes 393220

commit v2 on v1

v2 whole, which is shorter than its diff:
```python
import functools
import math
import jax
import jax.numpy as jnp
from jax import lax
from jax.experimental import pallas as pl
from jax.experimental.pallas import tpu as pltpu
from jax.sharding import PartitionSpec as P

HD = 128
SPLIT = 2
WINDOW = 3
CHUNK = 4
STACK = 2
MESH = pl.DeviceIdType.MESH
NT = (((1,), (1,)), ((), ()))


def kernel(
    n_ctx, n_head, group,
    q_ref, k_ref, v_ref, g_ref, doc_ref,
    dq_out, dk_out, dv_out,
    q_buf, g_buf, dq_buf, kv_buf, kt_buf, acc, bias, part_out, part_in, own_part, tot,
    own_sem, kv_send, kv_recv, ctx_send, ctx_recv, in_send, in_recv,
    dq_send, dq_recv, part_send, part_recv, tot_send, tot_recv,
):
    c = lax.axis_index("ctx")
    h = lax.axis_index("head")
    high = n_head // SPLIT
    low = h % SPLIT
    here = c * high + h // SPLIT
    n_blk = n_ctx * high
    back = WINDOW * high
    rows = q_ref.shape[0]
    blk = rows * SPLIT
    win = (back + 1) * blk
    kv_n = kv_buf.shape[0]
    n_chunk, _, width = q_buf.shape
    per_kv = n_chunk // kv_n
    cols = n_chunk * width
    scale = 1.0 / HD**0.5
    spread = range(1, back + 1)

    def peer(p):
        return (low + p) % SPLIT

    def mate(p):
        return (c, h - low + peer(p))

    def device(b):
        return (b // high, b % high * SPLIT + low)

    barrier = pltpu.get_barrier_semaphore()
    for p in range(1, SPLIT):
        pl.semaphore_signal(barrier, inc=1, device_id=mate(p), device_id_type=MESH)
    for s in spread:
        for b in ((here + s) % n_blk, (here - s + n_blk) % n_blk):
            pl.semaphore_signal(barrier, inc=1, device_id=device(b), device_id_type=MESH)
    pl.semaphore_wait(barrier, SPLIT - 1 + 2 * back)

    def at(n, size):
        return pl.ds(pl.multiple_of(n * size, size), size)

    def kv_copy(kv, t, p):
        to = peer(p)
        ref = (k_ref, v_ref)[t]
        return pltpu.make_async_remote_copy(
            src_ref=ref.at[:, at(to * kv_n + kv, HD)],
            dst_ref=kv_buf.at[kv, back, t, at(low, rows)],
            send_sem=kv_send.at[kv, t, p - 1],
            recv_sem=kv_recv.at[kv, t, p - 1],
            device_id=mate(p), device_id_type=MESH,
        )

    def kv_own(kv, t):
        ref = (k_ref, v_ref)[t]
        return pltpu.make_async_copy(
            ref.at[:, at(low * kv_n + kv, HD)], kv_buf.at[kv, back, t, at(low, rows)],
            own_sem.at[kv, t],
        )

    def in_copy(ch, t, p):
        to = peer(p)
        return pltpu.make_async_remote_copy(
            src_ref=(q_ref, g_ref)[t].at[:, at(to * n_chunk + ch, width)],
            dst_ref=(q_buf, g_buf)[t].at[ch, at(low, rows)],
            send_sem=in_send.at[ch, t, p - 1],
            recv_sem=in_recv.at[ch, t, p - 1],
            device_id=mate(p), device_id_type=MESH,
        )

    def in_own(ch, t):
        return pltpu.make_async_copy(
            (q_ref, g_ref)[t].at[:, at(low * n_chunk + ch, width)],
            (q_buf, g_buf)[t].at[ch, at(low, rows)],
            in_recv.at[ch, t, SPLIT - 1],
        )

    def ctx_copy(kv, s):
        return pltpu.make_async_remote_copy(
            src_ref=kv_buf.at[kv, back], dst_ref=kv_buf.at[kv, back - s],
            send_sem=ctx_send.at[kv, s - 1], recv_sem=ctx_recv.at[kv, s - 1],
            device_id=device((here + s) % n_blk), device_id_type=MESH,
        )

    def dq_copy(ch, p):
        to = peer(p)
        return pltpu.make_async_remote_copy(
            src_ref=dq_buf.at[ch, at(to, rows)],
            dst_ref=dq_out.at[:, at(low * n_chunk + ch, width)],
            send_sem=dq_send.at[ch, p - 1], recv_sem=dq_recv.at[ch, p - 1],
            device_id=mate(p), device_id_type=MESH,
        )

    def dq_own(ch):
        return pltpu.make_async_copy(
            dq_buf.at[ch, at(low, rows)], dq_out.at[:, at(low * n_chunk + ch, width)],
            dq_send.at[ch, SPLIT - 1],
        )

    def part_copy(kv, s):
        return pltpu.make_async_remote_copy(
            src_ref=part_out.at[kv, s - 1], dst_ref=part_in.at[kv, s - 1],
            send_sem=part_send.at[kv, s - 1], recv_sem=part_recv.at[kv, s - 1],
            device_id=device((here - s + n_blk) % n_blk), device_id_type=MESH,
        )

    def tot_copy(kv, t, p):
        to = peer(p)
        return pltpu.make_async_remote_copy(
            src_ref=tot.at[kv, t, at(to, rows)],
            dst_ref=(dk_out, dv_out)[t].at[:, at(low * kv_n + kv, HD)],
            send_sem=tot_send.at[kv, t, p - 1], recv_sem=tot_recv.at[kv, t, p - 1],
            device_id=mate(p), device_id_type=MESH,
        )

    def tot_own(kv, t):
        return pltpu.make_async_copy(
            tot.at[kv, t, at(low, rows)], (dk_out, dv_out)[t].at[:, at(low * kv_n + kv, HD)],
            tot_send.at[kv, t, SPLIT - 1],
        )

    others = range(1, SPLIT)
    for kv in range(kv_n):
        for t in range(2):
            for p in others:
                kv_copy(kv, t, p).start()
            kv_own(kv, t).start()

    @pl.loop(0, n_chunk)
    def _(ch):
        for t in range(2):
            for p in others:
                in_copy(ch, t, p).start()
            in_own(ch, t).start()

    for kv in range(kv_n):
        for t in range(2):
            kv_own(kv, t).wait()
            for p in others:
                kv_copy(kv, t, p).wait_recv()
        for s in spread:
            @pl.when(here + s < n_blk)
            def _():
                ctx_copy(kv, s).start()

            @pl.when(here < s)
            def _():
                kv_buf[kv, back - s] = jnp.zeros(kv_buf.shape[2:], kv_buf.dtype)

    query_doc = doc_ref[pl.ds(here, 1), :].astype(jnp.float32)
    for part in range(back + 1):
        key_row = doc_ref[pl.ds(jnp.maximum(here - back + part, 0), 1), :].astype(jnp.float32)
        key_doc = jnp.transpose(jnp.broadcast_to(key_row, (blk, blk)))
        j = lax.broadcasted_iota(jnp.int32, (blk, blk), 0) + part * blk
        i = lax.broadcasted_iota(jnp.int32, (blk, blk), 1)
        ok = (j > i) & (j <= i + back * blk) & (here - back + part >= 0)
        ok = ok & (key_doc == query_doc)
        bias[pl.ds(part * blk, blk)] = jnp.where(ok, 0.0, -1e30)

    def finish(kv):
        for s in spread:
            @pl.when(here + s < n_blk)
            def _():
                part_copy(kv, s).wait_recv()
                own_part[kv] += part_in[kv, s - 1].astype(jnp.float32)

        tot[kv] = own_part[kv].astype(jnp.bfloat16)
        for t in range(2):
            for p in others:
                tot_copy(kv, t, p).start()
            tot_own(kv, t).start()

    for kv in range(kv_n):
        for s in spread:
            @pl.when(here >= s)
            def _():
                ctx_copy(kv, s).wait_recv()

        keys = kv_buf[kv, :, 0].reshape(win, HD)
        kt_buf[...] = jnp.transpose(keys.astype(jnp.float32)).astype(jnp.bfloat16)
        acc[...] = jnp.zeros(acc.shape, acc.dtype)

        @pl.loop(0, per_kv)
        def _(step):
            ch = kv * per_kv + step
            for t in range(2):
                in_own(ch, t).wait()
                for p in others:
                    in_copy(ch, t, p).wait_recv()
            for a in range(0, width // HD, STACK):
                lanes = [pl.ds((a + k) * HD, HD) for k in range(STACK)]
                q = jnp.concatenate([q_buf[ch, :, at_a] for at_a in lanes], axis=0)
                g = jnp.concatenate([g_buf[ch, :, at_a] for at_a in lanes], axis=0)
                key_win = kv_buf[kv, :, 0].reshape(win, HD)
                val_win = kv_buf[kv, :, 1].reshape(win, HD)
                s_t = lax.dot_general(key_win, q, NT, preferred_element_type=jnp.float32)
                s_t = s_t + jnp.concatenate([bias[...]] * STACK, axis=1)
                top = jnp.max(s_t, axis=0, keepdims=True)
                e_t = jnp.exp2((s_t - top) * (scale * math.log2(math.e)))
                w_t = e_t * (1.0 / jnp.sum(e_t, axis=0, keepdims=True))
                w_bf = w_t.astype(jnp.bfloat16)
                p_t = lax.dot_general(val_win, g, NT, preferred_element_type=jnp.float32)
                delta = jnp.sum(w_bf.astype(jnp.float32) * p_t, axis=0, keepdims=True)
                d_t = (w_t * (p_t - delta)).astype(jnp.bfloat16)
                dv = jnp.dot(w_bf, g, preferred_element_type=jnp.float32)
                dk = jnp.dot(d_t, q, preferred_element_type=jnp.float32)
                acc[:, 0] += dk.reshape(back + 1, blk, HD)
                acc[:, 1] += dv.reshape(back + 1, blk, HD)
                dq_t = jnp.dot(kt_buf[...], d_t, preferred_element_type=jnp.float32)
                dq = jnp.transpose(dq_t * scale).astype(jnp.bfloat16)
                for k, at_a in enumerate(lanes):
                    dq_buf[ch, :, at_a] = dq[k * blk : (k + 1) * blk]
            for p in others:
                dq_copy(ch, p).start()
            dq_own(ch).start()

        for s in spread:
            part_out[kv, s - 1, 0] = (acc[back - s, 0] * scale).astype(jnp.bfloat16)
            part_out[kv, s - 1, 1] = acc[back - s, 1].astype(jnp.bfloat16)

            @pl.when(here >= s)
            def _():
                part_copy(kv, s).start()
        own_part[kv, 0] = acc[back, 0] * scale
        own_part[kv, 1] = acc[back, 1]
        if kv:
            finish(kv - 1)

    finish(kv_n - 1)

    @pl.loop(0, n_chunk)
    def _(ch):
        for t in range(2):
            for p in others:
                in_copy(ch, t, p).wait_send()
        for p in others:
            dq_copy(ch, p).wait()
        dq_own(ch).wait()

    for kv in range(kv_n):
        for t in range(2):
            for p in others:
                kv_copy(kv, t, p).wait_send()
                tot_copy(kv, t, p).wait()
            tot_own(kv, t).wait()
        for s in spread:
            @pl.when(here + s < n_blk)
            def _():
                ctx_copy(kv, s).wait_send()

            @pl.when(here >= s)
            def _():
                part_copy(kv, s).wait_send()


def body(queries, keys, values, out_grad, doc_ids):
    n_ctx, n_head = lax.axis_size("ctx"), lax.axis_size("head")
    rows, q_cols = queries.shape
    kv_cols = keys.shape[1]
    blk = rows * SPLIT
    kv_n = kv_cols // HD // SPLIT
    back = WINDOW * (n_head // SPLIT)
    group = q_cols // kv_cols
    chunk = math.gcd(CHUNK, group)
    width = chunk * HD
    n_chunk = kv_n * group // chunk
    win = back + 1
    bf, f32, dma = jnp.bfloat16, jnp.float32, pltpu.SemaphoreType.DMA
    far = pl.BlockSpec(memory_space=pl.ANY)
    near = pl.BlockSpec(memory_space=pltpu.VMEM)
    dq, dk, dv = pl.pallas_call(
        functools.partial(kernel, n_ctx, n_head, group),
        out_shape=(
            jax.ShapeDtypeStruct((rows, q_cols), bf),
            jax.ShapeDtypeStruct((rows, kv_cols), bf),
            jax.ShapeDtypeStruct((rows, kv_cols), bf),
        ),
        in_specs=[far, far, far, far, near],
        out_specs=(far, far, far),
        scratch_shapes=[
            pltpu.VMEM((n_chunk, blk, width), bf),
            pltpu.VMEM((n_chunk, blk, width), bf),
            pltpu.VMEM((n_chunk, blk, width), bf),
            pltpu.VMEM((kv_n, win, 2, blk, HD), bf),
            pltpu.VMEM((HD, win * blk), bf),
            pltpu.VMEM((win, 2, blk, HD), f32),
            pltpu.VMEM((win * blk, blk), f32),
            pltpu.VMEM((kv_n, back, 2, blk, HD), bf),
            pltpu.VMEM((kv_n, back, 2, blk, HD), bf),
            pltpu.VMEM((kv_n, 2, blk, HD), f32),
            pltpu.VMEM((kv_n, 2, blk, HD), bf),
            dma((kv_n, 2)),
            dma((kv_n, 2, SPLIT)),
            dma((kv_n, 2, SPLIT)),
            dma((kv_n, back)),
            dma((kv_n, back)),
            dma((n_chunk, 2, SPLIT)),
            dma((n_chunk, 2, SPLIT)),
            dma((n_chunk, SPLIT)),
            dma((n_chunk, SPLIT)),
            dma((kv_n, back)),
            dma((kv_n, back)),
            dma((kv_n, 2, SPLIT)),
            dma((kv_n, 2, SPLIT)),
        ],
        compiler_params=pltpu.CompilerParams(
            collective_id=0, has_side_effects=True, vmem_limit_bytes=56 * 2**20
        ),
    )(queries, keys, values, out_grad, doc_ids.reshape(-1, blk))
    return dq.astype(f32), dk.astype(f32), dv.astype(f32)


def solution(mesh):
    split = P(("ctx", "head"), None)
    return jax.shard_map(
        body,
        mesh=mesh,
        in_specs=(split, split, split, split, P()),
        out_specs=(split, split, split),
        check_vma=False,
    )
```

time: 62.1 us -> 69.4 us (1.12)
  Pallas kernels: 57 us -> 64.3 us
    pallas_call x1, Pallas kernels: 57 us -> 64.3 us  [body(): pl.pallas_call(functools.partial(kernel, n_ctx, n_head, group), out_shape...]
where the time goes in v2:
time: 69.4 us; the launch traced here: 69.1 us
  Pallas kernels  64.3 us (93%)
  other arithmetic  4.16 us (6%)
    pallas_call x1, Pallas kernels, body(): pl.pallas_call(functools.partial(kernel, n_ctx, n_head, group), out_shape...  64.3 us
    convert_element_type x3, other arithmetic, body(): return (dq.astype(f32), dk.astype(f32), dv.astype(f32))  4.16 us

profile of v2, /device:TPU:1, one launch (start us, length us, event | category | flops | bytes accessed | tf_op | source)
XLA Modules:
  0.0 69.1 jit_solution(17122347804287862997)
XLA Ops:
  0.6 64.3 %shard_map.76 = (bf16[64,8192]{1,0:T(8,128)(2,1)}, bf16[64,1024]{1,0:T(8,128)(2,1)}, bf16[64,1024]{1,0:T(8,128)(2,1)}) custom-call(bf16[64,8192]{1,0:T(8,128)(2,1)} %q_ref.1, bf16[64,1024]{1,0:T(8,128)(2,1)} %k_ref.1, bf16[64,1024]{1,0:T(8,128)(2,1)} %v_ref.1, bf16[64,8192]{1,0:T(8,128)(2,1)} %g_ref.1, s32[16,128]{1,0:T(8,128)} %bitcast.1), custom_call_target="tpu_custom_call" | custom-call | tf_op jit(solution)/shard_map/pallas_call | solution.py:292
  64.9 0.0 copy-start.1
  64.9 0.0 copy-start
  65.0 2.7 %convert_element_type.9 = f32[64,8192]{1,0:T(8,128)} convert(bf16[64,8192]{1,0:T(8,128)(2,1)} %get-tuple-element.6) | non-fusion elementwise | flops 524288 | bytes 3145728 | tf_op jit(solution)/shard_map/convert_element_type | solution.py:331
  67.7 0.0 copy-done.1
  67.7 0.7 %convert_element_type.10 = f32[64,1024]{1,0:T(8,128)} convert(bf16[64,1024]{1,0:T(8,128)(2,1)S(1)} %copy-done.1) | non-fusion elementwise | flops 65536 | bytes 393216 | tf_op jit(solution)/shard_map/convert_element_type | solution.py:331
  68.4 0.0 copy-done
  68.4 0.7 %convert_element_type.11 = f32[64,1024]{1,0:T(8,128)} convert(bf16[64,1024]{1,0:T(8,128)(2,1)S(1)} %copy-done) | non-fusion elementwise | flops 65536 | bytes 393216 | tf_op jit(solution)/shard_map/convert_element_type | solution.py:331
Async XLA Ops:
  64.9 2.7 %copy-start.1 = (bf16[64,1024]{1,0:T(8,128)(2,1)S(1)}, bf16[64,1024]{1,0:T(8,128)(2,1)}, u32[]{:S(2)}) copy-start(bf16[64,1024]{1,0:T(8,128)(2,1)} %get-tuple-element.7) | copy-start | bytes 393220
  64.9 3.5 %copy-start = (bf16[64,1024]{1,0:T(8,128)(2,1)S(1)}, bf16[64,1024]{1,0:T(8,128)(2,1)}, u32[]{:S(2)}) copy-start(bf16[64,1024]{1,0:T(8,128)(2,1)} %get-tuple-element.8) | copy-start | bytes 393220
